TPU v7x, 8 devices: a whole 2x2x1 slice. The times are simulated.
8 devices in a mesh: pz: 2 (over z, y), py: 4 (over x, core).
Axes of the slice: x: 2, y: 2, z: 1, core: 2. Of those that a mesh axis runs over, the one named last changes fastest.
Arguments:
- populations: float32 [19, 512, 32, 512], P(None, None, 'py', 'pz')
- relax_time: float32 [], replicated
- body_force: float32 [3], replicated
Outputs:
- output 1: float32 [19, 512, 32, 512], P(None, None, 'py', 'pz')
- output 2: float32 [512, 32, 512], P(None, 'py', 'pz')
- output 3: float32 [3, 512, 32, 512], P(None, None, 'py', 'pz')
All inputs are finite; a program needn't handle non-finite values.
Results may differ from a plain program's by a relative error of at most 0.001.
Values sent between devices are 32-bit elements.
A program may use at most 1 GiB of HBM per device.

v0:
```python
import jax
import jax.numpy as jnp
from jax import lax
from jax.sharding import PartitionSpec as P

STEPS = 4
VELOCITIES = ((0, 0, 0), (1, 0, 0), (-1, 0, 0), (0, 1, 0), (0, -1, 0), (0, 0, 1), (0, 0, -1), (1, 1, 0), (-1, -1, 0), (1, -1, 0), (-1, 1, 0), (1, 0, 1), (-1, 0, -1), (1, 0, -1), (-1, 0, 1), (0, 1, 1), (0, -1, -1), (0, 1, -1), (0, -1, 1))
WEIGHTS = (1.0 / 3.0,) + (1.0 / 18.0,) * 6 + (1.0 / 36.0,) * 12


def moments(populations, relax_time, body_force):
    density = jnp.sum(populations, axis=0)
    velocity = []
    for axis_id in range(3):
        plus_part = sum(populations[pop_id] for pop_id in range(19) if VELOCITIES[pop_id][axis_id] == 1)
        minus_part = sum(populations[pop_id] for pop_id in range(19) if VELOCITIES[pop_id][axis_id] == -1)
        velocity.append((plus_part - minus_part + body_force[axis_id] * relax_time) / density)
    return density, velocity


def equilibrium(density, velocity):
    speed_sq = velocity[0] * velocity[0] + velocity[1] * velocity[1] + velocity[2] * velocity[2]
    base_term = 1.0 - 1.5 * speed_sq
    result = []
    for pop_id in range(19):
        projection = sum(velocity[axis_id] * shift for axis_id, shift in enumerate(VELOCITIES[pop_id]) if shift != 0)
        result.append(WEIGHTS[pop_id] * density * (base_term + 3.0 * projection + 4.5 * projection * projection))
    return result


def collide(populations, relax_time, body_force):
    density, velocity = moments(populations, relax_time, body_force)
    feq_list = equilibrium(density, velocity)
    relax_rate = 1.0 / relax_time
    return jnp.stack([populations[pop_id] - (populations[pop_id] - feq_list[pop_id]) * relax_rate for pop_id in range(19)])


def neighbour_planes(block, axis_name, dim, depth, count):
    extent = block.shape[dim]
    upper = lax.slice_in_dim(block, extent - depth, extent, axis=dim)
    lower = lax.slice_in_dim(block, 0, depth, axis=dim)
    forward = [(source, (source + 1) % count) for source in range(count)]
    backward = [(source, (source - 1) % count) for source in range(count)]
    from_below = lax.ppermute(upper, axis_name, forward)
    from_above = lax.ppermute(lower, axis_name, backward)
    return jnp.concatenate([from_below, block, from_above], axis=dim)


def propagate_inner(padded):
    inner_y = padded.shape[2] - 2
    inner_z = padded.shape[3] - 2
    moved = []
    for pop_id in range(19):
        shift_x, shift_y, shift_z = VELOCITIES[pop_id]
        start_y = 1 - shift_y
        start_z = 1 - shift_z
        moved_pop = padded[pop_id, :, start_y:start_y + inner_y, start_z:start_z + inner_z]
        if shift_x != 0:
            moved_pop = jnp.roll(moved_pop, shift_x, axis=0)
        moved.append(moved_pop)
    return jnp.stack(moved)


def solution(mesh):
    size_y = mesh.shape["py"]
    size_z = mesh.shape["pz"]
    field_spec = P(None, None, "py", "pz")

    def local_steps(populations, relax_time, body_force):
        state = populations
        for step_id in range(STEPS):
            collided = collide(state, relax_time, body_force)
            collided = neighbour_planes(collided, "py", 2, 1, size_y)
            collided = neighbour_planes(collided, "pz", 3, 1, size_z)
            state = propagate_inner(collided)
        density, velocity = moments(state, relax_time, body_force)
        return state, density, jnp.stack(velocity)

    return jax.shard_map(local_steps, mesh=mesh, in_specs=(field_spec, P(), P()), out_specs=(field_spec, P(None, "py", "pz"), field_spec), check_vma=False)
```

profile of v0, /device:TPU:0, one launch (start us, length us, event | category | flops | bytes accessed | tf_op | source)
XLA Modules:
  0.0 3675.5 jit_solution(915105030949960278)
XLA Ops:
  161.5 56.5 %fusion.562 = (f32[19,512,1,256]{3,2,1,0:T(1,128)}, f32[19,512,1,256]{3,2,1,0:T(1,128)}) fusion(f32[19,512,8,256]{3,2,1,0:T(8,128)} %fusion.94), kind=kLoop, calls=%fused_computation.1025 | loop fusion | bytes 39845888 | tf_op jit(solution)/shard_map/slice | solution.py:40
  269.4 165.9 %collective-permute-done.1 = f32[19,512,1,256]{3,2,1,0:T(1,128)} collective-permute-done((f32[19,512,1,256]{3,2,1,0:T(1,128)}, f32[19,512,1,256]{3,2,1,0:T(1,128)}, u32[]{:S(2)}, u32[]{:S(2)}) %collective-permute-start.1) | collective-permute-done | bytes 9961504 | tf_op jit(solution)/shard_map/ppermute | solution.py:45
  436.3 86.7 %pad_maximum_fusion = f32[19,512,10,256]{3,2,1,0:T(8,128)} fusion(f32[19,512,1,256]{3,2,1,0:T(1,128)} %collective-permute-done.1, f32[19,512,8,256]{3,2,1,0:T(8,128)} %fusion.94, f32[19,512,1,256]{3,2,1,0:T(1,128)} %collective-permute-done), kind=kLoop, calls=%fused_computation | loop fusion | flops 49807360 | bytes 199229440 | tf_op jit(solution)/shard_map/concatenate | solution.py:46
  523.1 103.8 %fusion.558 = (f32[19,512,10,1]{3,2,1,0:T(8,128)}, f32[19,512,10,1]{3,2,1,0:T(8,128)}) fusion(f32[19,512,10,256]{3,2,1,0:T(8,128)} %pad_maximum_fusion), kind=kLoop, calls=%fused_computation.1021 | loop fusion | bytes 1556480 | tf_op jit(solution)/shard_map/slice | solution.py:41
  833.6 54.7 %fusion.99 = (f32[512,8,256]{2,1,0:T(8,128)}, f32[512,8,256]{2,1,0:T(8,128)}, f32[512,8,256]{2,1,0:T(8,128)}, f32[512,8,256]{2,1,0:T(8,128)}, f32[512,8,256]{2,1...) fusion(f32[]{:T(128)S(6)} %div.1200, ...), kind=kLoop, calls=%fused_computation.168 | loop fusion | flops 108003328 | bytes 209444880 | tf_op jit(solution)/shard_map/sub | solution.py:35
  998.0 56.8 %fusion.561 = (f32[19,512,1,256]{3,2,1,0:T(1,128)}, f32[19,512,1,256]{3,2,1,0:T(1,128)}) fusion(f32[19,512,8,256]{3,2,1,0:T(8,128)} %fusion.189), kind=kLoop, calls=%fused_computation.1024 | loop fusion | bytes 39845888 | tf_op jit(solution)/shard_map/slice | solution.py:40
  1071.4 198.4 %collective-permute-done.5 = f32[19,512,1,256]{3,2,1,0:T(1,128)} collective-permute-done((f32[19,512,1,256]{3,2,1,0:T(1,128)}, f32[19,512,1,256]{3,2,1,0:T(1,128)}, u32[]{:S(2)}, u32[]{:S(2)}) %collective-permute-start.5) | collective-permute-done | bytes 9961504 | tf_op jit(solution)/shard_map/ppermute | solution.py:45
  1271.3 86.3 %pad_maximum_fusion.1 = f32[19,512,10,256]{3,2,1,0:T(8,128)} fusion(f32[19,512,1,256]{3,2,1,0:T(1,128)} %collective-permute-done.5, f32[19,512,8,256]{3,2,1,0:T(8,128)} %fusion.189, f32[19,512,1,256]{3,2,1,0:T(1,128)} %collective-permute-done.4), kind=kLoop, calls=%fused_computation.1 | loop fusion | flops 49807360 | bytes 199229440 | tf_op jit(solution)/shard_map/concatenate | solution.py:46
  1357.6 103.8 %fusion.557 = (f32[19,512,10,1]{3,2,1,0:T(8,128)}, f32[19,512,10,1]{3,2,1,0:T(8,128)}) fusion(f32[19,512,10,256]{3,2,1,0:T(8,128)} %pad_maximum_fusion.1), kind=kLoop, calls=%fused_computation.1020 | loop fusion | bytes 1556480 | tf_op jit(solution)/shard_map/slice | solution.py:41
  1461.4 44.0 %copy.168 = f32[19,512,10,1]{1,3,2,0:T(1,128)S(1)} copy(f32[19,512,10,1]{3,2,1,0:T(8,128)} %get-tuple-element.121) | data formatting | bytes 778240 | tf_op jit(solution)/shard_map/slice | solution.py:40
  1666.5 53.3 %fusion.194 = (f32[512,8,256]{2,1,0:T(8,128)}, f32[512,8,256]{2,1,0:T(8,128)}, f32[512,8,256]{2,1,0:T(8,128)}, f32[512,8,256]{2,1,0:T(8,128)}, f32[1,512,8,256]{...) fusion(f32[]{:T(128)S(6)} %div.1200, ...), kind=kLoop, calls=%fused_computation.263 | loop fusion | flops 108003328 | bytes 205250576 | tf_op jit(solution)/shard_map/sub | solution.py:35
  1719.9 75.4 %constant_dynamic-update-slice_fusion.2 = (f32[19,512,8,256]{3,2,1,0:T(8,128)}, f32[1,512,8,256]{3,2,1,0:T(8,128)}, f32[1,512,8,256]{3,2,1,0:T(8,128)}, f32[1,51...) fusion(f32[1,512,8,256]{3,2,1,0:T(8,128)} %get-tuple-element.79, ...), kind=kLoop, calls=%fused_computation.959 | loop fusion | flops 168820736 | bytes 239075344
  1869.6 57.2 %fusion.560 = (f32[19,512,1,256]{3,2,1,0:T(1,128)}, f32[19,512,1,256]{3,2,1,0:T(1,128)}) fusion(f32[19,512,8,256]{3,2,1,0:T(8,128)} %fusion.284), kind=kLoop, calls=%fused_computation.1023 | loop fusion | bytes 39845888 | tf_op jit(solution)/shard_map/slice | solution.py:40
  1942.2 199.1 %collective-permute-done.9 = f32[19,512,1,256]{3,2,1,0:T(1,128)} collective-permute-done((f32[19,512,1,256]{3,2,1,0:T(1,128)}, f32[19,512,1,256]{3,2,1,0:T(1,128)}, u32[]{:S(2)}, u32[]{:S(2)}) %collective-permute-start.9) | collective-permute-done | bytes 9961504 | tf_op jit(solution)/shard_map/ppermute | solution.py:45
  2143.1 86.3 %pad_maximum_fusion.2 = f32[19,512,10,256]{3,2,1,0:T(8,128)} fusion(f32[19,512,1,256]{3,2,1,0:T(1,128)} %collective-permute-done.9, f32[19,512,8,256]{3,2,1,0:T(8,128)} %fusion.284, f32[19,512,1,256]{3,2,1,0:T(1,128)} %collective-permute-done.8), kind=kLoop, calls=%fused_computation.2 | loop fusion | flops 49807360 | bytes 199229440 | tf_op jit(solution)/shard_map/concatenate | solution.py:46
  2229.5 103.8 %fusion.556 = (f32[19,512,10,1]{3,2,1,0:T(8,128)}, f32[19,512,10,1]{3,2,1,0:T(8,128)}) fusion(f32[19,512,10,256]{3,2,1,0:T(8,128)} %pad_maximum_fusion.2), kind=kLoop, calls=%fused_computation.1019 | loop fusion | bytes 1556480 | tf_op jit(solution)/shard_map/slice | solution.py:41
  2538.2 56.2 %multiply_subtract_fusion = (f32[512,8,256]{2,1,0:T(8,128)}, f32[512,8,256]{2,1,0:T(8,128)}, f32[512,8,256]{2,1,0:T(8,128)}, f32[512,8,256]{2,1,0:T(8,128)}, f32...) fusion(f32[]{:T(128)S(6)} %div.1200, ...), kind=kLoop, calls=%fused_computation.871 | loop fusion | flops 114294784 | bytes 217833488 | tf_op jit(solution)/shard_map/sub | solution.py:35
  2594.6 73.3 %multiply_subtract_fusion.2 = (f32[1,512,8,256]{3,2,1,0:T(8,128)}, f32[1,512,8,256]{3,2,1,0:T(8,128)}, f32[1,512,8,256]{3,2,1,0:T(8,128)}, f32[1,512,8,256]{3,2,...) fusion(f32[1,512,8,256]{3,2,1,0:T(8,128)} %get-tuple-element.49, ...), kind=kLoop, calls=%fused_computation.875 | loop fusion | flops 163577856 | bytes 230686736 | tf_op jit(solution)/shard_map/sub | solution.py:35
  2672.3 51.1 %copy.252 = f32[19,512,8,256]{3,2,1,0:T(8,128)} copy(f32[19,512,8,256]{3,2,1,0:T(8,128)} %constant_dynamic-update-slice_fusion.12) | data formatting | bytes 159383552
  2798.1 56.3 %fusion.559 = (f32[19,512,1,256]{3,2,1,0:T(1,128)}, f32[19,512,1,256]{3,2,1,0:T(1,128)}) fusion(f32[19,512,8,256]{3,2,1,0:T(8,128)} %fusion.379), kind=kLoop, calls=%fused_computation.1022 | loop fusion | bytes 39845888 | tf_op jit(solution)/shard_map/slice | solution.py:40
  2875.3 193.1 %collective-permute-done.13 = f32[19,512,1,256]{3,2,1,0:T(1,128)} collective-permute-done((f32[19,512,1,256]{3,2,1,0:T(1,128)}, f32[19,512,1,256]{3,2,1,0:T(1,128)}, u32[]{:S(2)}, u32[]{:S(2)}) %collective-permute-start.13) | collective-permute-done | bytes 9961504 | tf_op jit(solution)/shard_map/ppermute | solution.py:45
  3070.5 85.7 %pad_maximum_fusion.3 = f32[19,512,10,256]{3,2,1,0:T(8,128)} fusion(f32[19,512,1,256]{3,2,1,0:T(1,128)} %collective-permute-done.13, f32[19,512,8,256]{3,2,1,0:T(8,128)} %fusion.379, f32[19,512,1,256]{3,2,1,0:T(1,128)} %collective-permute-done.12), kind=kLoop, calls=%fused_computation.3 | loop fusion | flops 49807360 | bytes 199229440 | tf_op jit(solution)/shard_map/concatenate | solution.py:46
  3156.2 103.8 %fusion.555 = (f32[19,512,10,1]{3,2,1,0:T(8,128)}, f32[19,512,10,1]{3,2,1,0:T(8,128)}) fusion(f32[19,512,10,256]{3,2,1,0:T(8,128)} %pad_maximum_fusion.3), kind=kLoop, calls=%fused_computation.1018 | loop fusion | bytes 1556480 | tf_op jit(solution)/shard_map/slice | solution.py:41
  3461.6 85.9 %fusion.385 = (f32[1,512,8,256]{3,2,1,0:T(8,128)}, f32[1,512,8,256]{3,2,1,0:T(8,128)}, f32[1,512,8,256]{3,2,1,0:T(8,128)}, f32[1,512,8,256]{3,2,1,0:T(8,128)}, f...) fusion(f32[1,511,8,256]{3,2,1,0:T(8,128)} %get-tuple-element.19, ...), kind=kLoop, calls=%fused_computation.573 | loop fusion | flops 148897792 | bytes 305913856 | tf_op jit(solution)/shard_map/div | solution.py:17
  (509 shorter events, 1432.7 us)
Async XLA Ops:
  218.0 217.3 %collective-permute-start.1 = (f32[19,512,1,256]{3,2,1,0:T(1,128)}, f32[19,512,1,256]{3,2,1,0:T(1,128)}, u32[]{:S(2)}, u32[]{:S(2)}) collective-permute-start(f32[19,512,1,256]{3,2,1,0:T(1,128)} %get-tuple-element.179), channel_id=1, source_target_pairs={{0,3},{1,0},{2,1},{3,2},{4,7},{5,4},{6,5},{7,6}} | collective-permute-start | bytes 29884424 | tf_op jit(solution)/shard_map/ppermute | solution.py:45
  220.8 215.6 %collective-permute-start = (f32[19,512,1,256]{3,2,1,0:T(1,128)}, f32[19,512,1,256]{3,2,1,0:T(1,128)}, u32[]{:S(2)}, u32[]{:S(2)}) collective-permute-start(f32[19,512,1,256]{3,2,1,0:T(1,128)} %get-tuple-element.178), channel_id=1, source_target_pairs={{0,1},{1,2},{2,3},{3,0},{4,5},{5,6},{6,7},{7,4}} | collective-permute-start | bytes 29884424 | tf_op jit(solution)/shard_map/ppermute | solution.py:44
  670.8 57.5 %collective-permute-start.2 = (f32[19,512,10,1]{1,3,2,0:T(1,128)S(1)}, f32[19,512,10,1]{1,3,2,0:T(1,128)S(1)}, u32[]{:S(2)}, u32[]{:S(2)}) collective-permute-start(f32[19,512,10,1]{1,3,2,0:T(1,128)S(1)} %copy.164), channel_id=1, source_target_pairs={{0,4},{4,0},{1,5},{5,1},{2,6},{6,2},{3,7},{7,3}} | collective-permute-start | bytes 1167368 | tf_op jit(solution)/shard_map/ppermute | solution.py:44
  716.4 50.2 %collective-permute-start.3 = (f32[19,512,10,1]{1,3,2,0:T(1,128)S(1)}, f32[19,512,10,1]{1,3,2,0:T(1,128)S(1)}, u32[]{:S(2)}, u32[]{:S(2)}) collective-permute-start(f32[19,512,10,1]{1,3,2,0:T(1,128)S(1)} %copy.166), channel_id=1, source_target_pairs={{0,4},{4,0},{1,5},{5,1},{2,6},{6,2},{3,7},{7,3}} | collective-permute-start | bytes 1167368 | tf_op jit(solution)/shard_map/ppermute | solution.py:45
  1054.8 215.0 %collective-permute-start.5 = (f32[19,512,1,256]{3,2,1,0:T(1,128)}, f32[19,512,1,256]{3,2,1,0:T(1,128)}, u32[]{:S(2)}, u32[]{:S(2)}) collective-permute-start(f32[19,512,1,256]{3,2,1,0:T(1,128)} %get-tuple-element.175), channel_id=1, source_target_pairs={{0,3},{1,0},{2,1},{3,2},{4,7},{5,4},{6,5},{7,6}} | collective-permute-start | bytes 29884424 | tf_op jit(solution)/shard_map/ppermute | solution.py:45
  1055.5 215.8 %collective-permute-start.4 = (f32[19,512,1,256]{3,2,1,0:T(1,128)}, f32[19,512,1,256]{3,2,1,0:T(1,128)}, u32[]{:S(2)}, u32[]{:S(2)}) collective-permute-start(f32[19,512,1,256]{3,2,1,0:T(1,128)} %get-tuple-element.174), channel_id=1, source_target_pairs={{0,1},{1,2},{2,3},{3,0},{4,5},{5,6},{6,7},{7,4}} | collective-permute-start | bytes 29884424 | tf_op jit(solution)/shard_map/ppermute | solution.py:44
  1505.4 57.4 %collective-permute-start.6 = (f32[19,512,10,1]{1,3,2,0:T(1,128)S(1)}, f32[19,512,10,1]{1,3,2,0:T(1,128)S(1)}, u32[]{:S(2)}, u32[]{:S(2)}) collective-permute-start(f32[19,512,10,1]{1,3,2,0:T(1,128)S(1)} %copy.168), channel_id=1, source_target_pairs={{0,4},{4,0},{1,5},{5,1},{2,6},{6,2},{3,7},{7,3}} | collective-permute-start | bytes 1167368 | tf_op jit(solution)/shard_map/ppermute | solution.py:44
  1550.9 50.1 %collective-permute-start.7 = (f32[19,512,10,1]{1,3,2,0:T(1,128)S(1)}, f32[19,512,10,1]{1,3,2,0:T(1,128)S(1)}, u32[]{:S(2)}, u32[]{:S(2)}) collective-permute-start(f32[19,512,10,1]{1,3,2,0:T(1,128)S(1)} %copy.170), channel_id=1, source_target_pairs={{0,4},{4,0},{1,5},{5,1},{2,6},{6,2},{3,7},{7,3}} | collective-permute-start | bytes 1167368 | tf_op jit(solution)/shard_map/ppermute | solution.py:45
  1664.4 181.1 %copy-start.95 = (f32[1,1,8,256]{3,2,1,0:T(8,128)}, f32[1,1,8,256]{3,2,1,0:T(8,128)S(1)}, u32[]{:S(2)}) copy-start(f32[1,1,8,256]{3,2,1,0:T(8,128)S(1)} %get-tuple-element.132) | copy-start | bytes 24580
  1664.4 184.6 %copy-start.97 = (f32[1,1,8,256]{3,2,1,0:T(8,128)}, f32[1,1,8,256]{3,2,1,0:T(8,128)S(1)}, u32[]{:S(2)}) copy-start(f32[1,1,8,256]{3,2,1,0:T(8,128)S(1)} %get-tuple-element.133) | copy-start | bytes 24580
  1664.4 189.5 %copy-start.93 = (f32[1,1,8,256]{3,2,1,0:T(8,128)}, f32[1,1,8,256]{3,2,1,0:T(8,128)S(1)}, u32[]{:S(2)}) copy-start(f32[1,1,8,256]{3,2,1,0:T(8,128)S(1)} %get-tuple-element.101) | copy-start | bytes 24580
  1926.8 214.5 %collective-permute-start.9 = (f32[19,512,1,256]{3,2,1,0:T(1,128)}, f32[19,512,1,256]{3,2,1,0:T(1,128)}, u32[]{:S(2)}, u32[]{:S(2)}) collective-permute-start(f32[19,512,1,256]{3,2,1,0:T(1,128)} %get-tuple-element.171), channel_id=1, source_target_pairs={{0,3},{1,0},{2,1},{3,2},{4,7},{5,4},{6,5},{7,6}} | collective-permute-start | bytes 29884424 | tf_op jit(solution)/shard_map/ppermute | solution.py:45
  1927.2 216.0 %collective-permute-start.8 = (f32[19,512,1,256]{3,2,1,0:T(1,128)}, f32[19,512,1,256]{3,2,1,0:T(1,128)}, u32[]{:S(2)}, u32[]{:S(2)}) collective-permute-start(f32[19,512,1,256]{3,2,1,0:T(1,128)} %get-tuple-element.170), channel_id=1, source_target_pairs={{0,1},{1,2},{2,3},{3,0},{4,5},{5,6},{6,7},{7,4}} | collective-permute-start | bytes 29884424 | tf_op jit(solution)/shard_map/ppermute | solution.py:44
  2377.2 57.5 %collective-permute-start.10 = (f32[19,512,10,1]{1,3,2,0:T(1,128)S(1)}, f32[19,512,10,1]{1,3,2,0:T(1,128)S(1)}, u32[]{:S(2)}, u32[]{:S(2)}) collective-permute-start(f32[19,512,10,1]{1,3,2,0:T(1,128)S(1)} %copy.172), channel_id=1, source_target_pairs={{0,4},{4,0},{1,5},{5,1},{2,6},{6,2},{3,7},{7,3}} | collective-permute-start | bytes 1167368 | tf_op jit(solution)/shard_map/ppermute | solution.py:44
  2422.8 50.2 %collective-permute-start.11 = (f32[19,512,10,1]{1,3,2,0:T(1,128)S(1)}, f32[19,512,10,1]{1,3,2,0:T(1,128)S(1)}, u32[]{:S(2)}, u32[]{:S(2)}) collective-permute-start(f32[19,512,10,1]{1,3,2,0:T(1,128)S(1)} %copy.174), channel_id=1, source_target_pairs={{0,4},{4,0},{1,5},{5,1},{2,6},{6,2},{3,7},{7,3}} | collective-permute-start | bytes 1167368 | tf_op jit(solution)/shard_map/ppermute | solution.py:45
  2536.2 220.6 %copy-start.131 = (f32[1,1,8,256]{3,2,1,0:T(8,128)}, f32[1,1,8,256]{3,2,1,0:T(8,128)S(1)}, u32[]{:S(2)}) copy-start(f32[1,1,8,256]{3,2,1,0:T(8,128)S(1)} %get-tuple-element.146) | copy-start | bytes 24580
  2536.2 234.6 %copy-start.123 = (f32[1,1,8,256]{3,2,1,0:T(8,128)}, f32[1,1,8,256]{3,2,1,0:T(8,128)S(1)}, u32[]{:S(2)}) copy-start(f32[1,1,8,256]{3,2,1,0:T(8,128)S(1)} %get-tuple-element.92) | copy-start | bytes 24580
  2536.2 237.8 %copy-start.127 = (f32[1,1,8,256]{3,2,1,0:T(8,128)}, f32[1,1,8,256]{3,2,1,0:T(8,128)S(1)}, u32[]{:S(2)}) copy-start(f32[1,1,8,256]{3,2,1,0:T(8,128)S(1)} %get-tuple-element.128) | copy-start | bytes 24580
  2536.2 241.3 %copy-start.129 = (f32[1,1,8,256]{3,2,1,0:T(8,128)}, f32[1,1,8,256]{3,2,1,0:T(8,128)S(1)}, u32[]{:S(2)}) copy-start(f32[1,1,8,256]{3,2,1,0:T(8,128)S(1)} %get-tuple-element.129) | copy-start | bytes 24580
  2536.3 246.2 %copy-start.125 = (f32[1,1,8,256]{3,2,1,0:T(8,128)}, f32[1,1,8,256]{3,2,1,0:T(8,128)S(1)}, u32[]{:S(2)}) copy-start(f32[1,1,8,256]{3,2,1,0:T(8,128)S(1)} %get-tuple-element.93) | copy-start | bytes 24580
  2854.4 214.0 %collective-permute-start.13 = (f32[19,512,1,256]{3,2,1,0:T(1,128)}, f32[19,512,1,256]{3,2,1,0:T(1,128)}, u32[]{:S(2)}, u32[]{:S(2)}) collective-permute-start(f32[19,512,1,256]{3,2,1,0:T(1,128)} %get-tuple-element.167), channel_id=1, source_target_pairs={{0,3},{1,0},{2,1},{3,2},{4,7},{5,4},{6,5},{7,6}} | collective-permute-start | bytes 29884424 | tf_op jit(solution)/shard_map/ppermute | solution.py:45
  2854.4 216.1 %collective-permute-start.12 = (f32[19,512,1,256]{3,2,1,0:T(1,128)}, f32[19,512,1,256]{3,2,1,0:T(1,128)}, u32[]{:S(2)}, u32[]{:S(2)}) collective-permute-start(f32[19,512,1,256]{3,2,1,0:T(1,128)} %get-tuple-element.166), channel_id=1, source_target_pairs={{0,1},{1,2},{2,3},{3,0},{4,5},{5,6},{6,7},{7,4}} | collective-permute-start | bytes 29884424 | tf_op jit(solution)/shard_map/ppermute | solution.py:44
  3304.0 54.4 %collective-permute-start.14 = (f32[19,512,10,1]{1,3,2,0:T(1,128)S(1)}, f32[19,512,10,1]{1,3,2,0:T(1,128)S(1)}, u32[]{:S(2)}, u32[]{:S(2)}) collective-permute-start(f32[19,512,10,1]{1,3,2,0:T(1,128)S(1)} %copy.176), channel_id=1, source_target_pairs={{0,4},{4,0},{1,5},{5,1},{2,6},{6,2},{3,7},{7,3}} | collective-permute-start | bytes 1167368 | tf_op jit(solution)/shard_map/ppermute | solution.py:44
  3346.6 50.1 %collective-permute-start.15 = (f32[19,512,10,1]{1,0,3,2:T(8,128)S(1)}, f32[19,512,10,1]{1,0,3,2:T(8,128)S(1)}, u32[]{:S(2)}, u32[]{:S(2)}) collective-permute-start(f32[19,512,10,1]{1,0,3,2:T(8,128)S(1)} %copy.178), channel_id=1, source_target_pairs={{0,4},{4,0},{1,5},{5,1},{2,6},{6,2},{3,7},{7,3}} | collective-permute-start | bytes 1167368 | tf_op jit(solution)/shard_map/ppermute | solution.py:45
  (159 other events, 3746.0 us)
where the time goes:
time: 3690 us; the launch traced here: 3680 us
  local copies, waits for them, and re-layouts  1460 us (40%)
  other arithmetic  1440 us (39%)
  waiting for transfers between devices  763 us (21%)
    ppermute x8, waiting for transfers between devices, neighbour_planes(): from_above = lax.ppermute(lower, axis_name, backward)  757 us
    slice x8, local copies, waits for them, and re-layouts, neighbour_planes(): lower = lax.slice_in_dim(block, 0, depth, axis=dim)  588 us
    unnamed x81, other arithmetic  448 us
    slice x8, local copies, waits for them, and re-layouts, neighbour_planes(): upper = lax.slice_in_dim(block, extent - depth, extent, axis=dim)  403 us
    concatenate x4, other arithmetic, neighbour_planes(): return jnp.concatenate([from_below, block, from_above], axis=dim)  345 us
    sub x9, other arithmetic, collide(): populations[pop_id] - (populations[pop_id] - feq_list[pop_id]) * relax_rate  290 us
    ppermute x4, local copies, waits for them, and re-layouts, neighbour_planes(): from_below = lax.ppermute(upper, axis_name, forward)  153 us
    ppermute x4, local copies, waits for them, and re-layouts, neighbour_planes(): from_above = lax.ppermute(lower, axis_name, backward)  151 us
  transfers between devices with their start and end apart: 16, of which 8 were waited for; matrix products, arithmetic and copies ran while one was open for 13% of the time, Pallas kernels for 0%

commit v1 on v0

v1 whole, which is shorter than its diff:
```python
import functools

import jax
import jax.numpy as jnp
from jax import lax
from jax.experimental import pallas as pl
from jax.experimental.pallas import tpu as pltpu
from jax.sharding import PartitionSpec as P


MESH = pl.DeviceIdType.MESH
STEPS = 4
FORWARD = ((1, 0, 0), (0, 1, 0), (0, 0, 1), (1, 1, 0), (1, -1, 0), (1, 0, 1), (1, 0, -1), (0, 1, 1), (0, 1, -1))
VELOCITIES = ((0, 0, 0),) + tuple(tuple(sign * c for c in way) for way in FORWARD for sign in (1, -1))

STILL = tuple(p for p in range(19) if VELOCITIES[p][1] == 0)
UP = tuple(p for p in range(19) if VELOCITIES[p][1] == 1)
DOWN = tuple(p for p in range(19) if VELOCITIES[p][1] == -1)
ZPAIRS = tuple(
    (p, q) for p in range(19) for q in range(19)
    if VELOCITIES[p][2] == 1 and VELOCITIES[q] == VELOCITIES[p][:2] + (-1,))

C = 8
NS = 8
LAG = 3
RP = C * NS
LOOK = 2
NZ = 16
ZLAG = 6
PIECES = (10, 10, 12, 16, 16)
GROUP_ROWS = 2 * 5 * C * 2 + 8 + 2
Z_ROWS = 8 + 2
VMEM_BYTES = 62 * 2 ** 20


TILE = (8, 128)
GROUPS = (len(STILL), len(UP), len(DOWN))
F32 = jnp.float32


def splat(value):
    return jnp.full(TILE, value, F32)


def ring(pops, planes, *rows):
    return pltpu.VMEM((pops, planes, 2) + (rows or TILE[:1]) + TILE[1:], F32)


def sums(f, tau_g):
    s = {}
    d = {}
    for p in range(1, 19, 2):
        s[p] = f[p] + f[p + 1]
        d[p] = f[p] - f[p + 1]
    rho = f[0] + ((s[1] + s[3]) + (s[5] + s[7])) + ((s[9] + s[11]) + (s[13] + s[15])) + s[17]
    jx = (d[1] + (d[7] + d[9])) + ((d[11] + d[13]) + tau_g[0])
    jy = (d[3] + (d[7] - d[9])) + ((d[15] + d[17]) + tau_g[1])
    jz = (d[5] + (d[11] - d[13])) + ((d[15] - d[17]) + tau_g[2])
    return rho, (jx, jy, jz), s, d


def forced_moments(f, tau_g):
    rho, momentum, _, _ = sums(f, tau_g)
    inv = 1.0 / rho
    return rho, tuple(j * inv for j in momentum)


def collide(f, tau_g, rate36, keep, half_keep):
    rho, momentum, s, d = sums(f, tau_g)
    inv3 = 3.0 / rho
    u3 = tuple(j * inv3 for j in momentum)
    rw = rate36 * rho
    odd = tuple(rw * u for u in u3)
    square = tuple(u * o for u, o in zip(u3, odd))
    pair_square = {(0, 1): square[0] + square[1], (0, 2): square[0] + square[2], (1, 2): square[1] + square[2]}
    even = rw - (pair_square[0, 1] + square[2]) * (1.0 / 6.0)
    even2 = even + even
    out = [None] * 19
    out[0] = keep * f[0] + 12.0 * even

    def relax(p, e, o):
        e = half_keep * s[p] + e
        o = half_keep * d[p] + o
        out[p] = e + o
        out[p + 1] = e - o

    for axis in range(3):
        relax(2 * axis + 1, even2 + square[axis], odd[axis] + odd[axis])
    for p, (a, b) in ((7, (0, 1)), (11, (0, 2)), (15, (1, 2))):
        mean = even + 0.5 * pair_square[a, b]
        cross = u3[a] * odd[b]
        relax(p, mean + cross, odd[a] + odd[b])
        relax(p + 2, mean - cross, odd[a] - odd[b])
    return out


def pull(still, up, down, zhalo, planes, lanes):
    halves = ([None] * 19, [None] * 19)
    edges = {}
    for p in range(19):
        cx, cy, cz = VELOCITIES[p]
        plane, place = planes[cx]
        if cy == 0:
            lo, hi = (still[STILL.index(p), plane, h] for h in range(2))
        elif cy == 1:
            lo, hi = (up[UP.index(p), plane, h, 7:15, :] for h in range(2))
        else:
            lo, hi = (down[DOWN.index(p), plane, h, 1:9, :] for h in range(2))
        if cz != 0:
            if p in edges:
                edge = edges[p]
            else:
                pair = next(n for n, pops in enumerate(ZPAIRS) if p in pops)
                edge = turn(zhalo(cx, slice(8 - cy, 16 - cy)), 127 - 2 * (pair * C + place))
                edges.update((pop, edge) for pop in ZPAIRS[pair])
            if cz == 1:
                lo = jnp.where(lanes == 0, edge, lo)
            else:
                hi = jnp.where(lanes == 127, edge, hi)
        halves[0][p] = lo
        halves[1][p] = hi
    return halves


def turn(value, amount):
    return pltpu.roll(value, amount, 1) if amount % 128 else value


def push(halves, lanes):
    column = None
    for n, (p, q) in enumerate(ZPAIRS):
        lo, hi = turn(halves[0][p], 1), turn(halves[1][p], 1)
        halves[0][p], halves[1][p] = lo, jnp.where(lanes == 0, lo, hi)
        back_lo, back_hi = turn(halves[0][q], 127), turn(halves[1][q], 127)
        halves[0][q], halves[1][q] = jnp.where(lanes == 127, back_hi, back_lo), back_hi
        leaving = turn(jnp.where(lanes == 0, hi, back_lo), 2 * n * C + 1)
        column = leaving if column is None else jnp.where(lanes >= 2 * n * C, leaving, column)
    return column


def march_kernel(
    chunks, tau_ref, force_ref, pops, *refs,
):
    g_still, g_up, g_down, z_halo = refs[:4]
    faces = refs[4:4 + 2 * len(PIECES)]
    (buf_in, rings, out_still, out_up, out_down, out_z, in_z,
    in_sem, out_sem, face_sem, send_sem, recv_sem, zsend_sem, zrecv_sem, ysend_sem, yrecv_sem, tally,
    ) = refs[4 + 2 * len(PIECES):]
    still, up, down, zsend, zrecv = rings
    py, pz = lax.axis_index("py"), lax.axis_index("pz")
    py_up, py_down, pz_other = lax.rem(py + 1, 4), lax.rem(py + 3, 4), 1 - pz
    above = {"py": py_up, "pz": pz}
    below = {"py": py_down, "pz": pz}
    beside = {"py": py, "pz": pz_other}
    corner_above = {"py": py_up, "pz": pz_other}
    corner_below = {"py": py_down, "pz": pz_other}
    in_z[...] = jnp.zeros_like(in_z)
    barrier = pltpu.get_barrier_semaphore()
    for peer in (above, below, beside, corner_above, corner_below):
        pl.semaphore_signal(barrier, inc=1, device_id=peer, device_id_type=MESH)

    def load(k, slot):
        return pltpu.make_async_copy(
            pops.at[:, pl.ds(lax.rem(k, chunks) * C, C)], buf_in.at[slot], in_sem.at[slot])

    load(0, 0).start()
    load(1, 1).start()

    tau = splat(tau_ref[0])
    rate = 1.0 / tau
    keep = 1.0 - rate
    half_keep = 0.5 * keep
    rate36 = rate * (1.0 / 36.0)
    tau_g = tuple(tau * force_ref[axis] for axis in range(3))
    lanes = lax.broadcasted_iota(jnp.int32, TILE, 1)
    places = lanes & (2 * C - 1)

    def sends(s, slot):
        rows = pl.ds(slot * C, C)
        pairs = (
            (up[s].at[:, rows, :, 15], up[s].at[:, rows, :, 7], above),
            (down[s].at[:, rows, :, 0], down[s].at[:, rows, :, 8], below),
            (zsend[s].at[slot], zrecv[s].at[slot, 8:16], beside),
            (zsend[s].at[slot, 7:8], zrecv[s].at[slot, 7:8], corner_above),
            (zsend[s].at[slot, 0:1], zrecv[s].at[slot, 16:17], corner_below),
        )
        return [
            pltpu.make_async_remote_copy(
                src_ref=src, dst_ref=dst, send_sem=send_sem.at[s, slot], recv_sem=recv_sem.at[s, slot],
                device_id=peer, device_id_type=MESH)
            for src, dst, peer in pairs
        ]

    def settle(sem, rows):
        pltpu.make_async_copy(tally.at[:rows], tally.at[:rows], sem).wait()

    def writes(k, slot):
        rows = pl.ds(k * C, C)
        pairs = (
            (out_still.at[slot], g_still.at[:, rows]),
            (out_up.at[slot], g_up.at[:, rows]),
            (out_down.at[slot], g_down.at[:, rows]),
        )
        return [pltpu.make_async_copy(src, dst, out_sem.at[slot, n]) for n, (src, dst) in enumerate(pairs)]

    def face_moves(k, act, pieces=len(PIECES)):
        slot = lax.rem(k, 2)
        for n, low, high, base in face_spans(chunks):
            if n >= pieces:
                continue

            def move(n=n, base=base):
                rows = pl.ds((k - base) * C, C)
                pairs = (
                    (out_up.at[slot, :, :, :, 7], faces[2 * n].at[:, rows], above),
                    (out_down.at[slot, :, :, :, 0], faces[2 * n + 1].at[:, rows], below),
                )
                for m, (face, dst, peer) in enumerate(pairs):
                    if n:
                        act(pltpu.make_async_copy(face, dst, face_sem.at[slot, n % 2, m]), False)
                    else:
                        act(pltpu.make_async_remote_copy(
                            src_ref=face, dst_ref=dst, send_sem=ysend_sem.at[slot, m], recv_sem=yrecv_sem.at[k, m],
                            device_id=peer, device_id_type=MESH), True)

            pl.when((k >= low) & (k < high))(move)

    def face_reclaim(k):
        face_moves(k, lambda copy, remote: copy.wait_send() if remote else copy.wait())

    def z_sends(k):
        slot = lax.rem(k, NZ)
        pairs = (
            (out_z.at[slot], in_z.at[k, 8:16], beside),
            (out_z.at[slot, 7:8], in_z.at[k, 7:8], corner_above),
            (out_z.at[slot, 0:1], in_z.at[k, 16:17], corner_below),
        )
        return [
            pltpu.make_async_remote_copy(
                src_ref=src, dst_ref=dst, send_sem=zsend_sem.at[slot], recv_sem=zrecv_sem.at[slot],
                device_id=peer, device_id_type=MESH)
            for src, dst, peer in pairs
        ]

    def fetch(s, k, j):
        slot = lax.rem(k, NS)
        if s == 0:
            return [
                [buf_in[lax.rem(k, 2), p, j, :, 128 * h:128 * h + 128] for p in range(19)] for h in range(2)]
        planes = {}
        slots = {}
        for cx in (1, 0, -1):
            ahead, place = divmod(j + 1 - cx, C)
            slots[cx] = slot if ahead == 0 else lax.rem(k + 1, NS)
            planes[cx] = (slots[cx] * C + place, place)
        zhalo = lambda cx, rows: zrecv[s - 1][slots[cx], rows, :]
        return pull(still[s - 1], up[s - 1], down[s - 1], zhalo, planes, lanes)

    def keep_plane(s, k, j, halves):
        at = lax.rem(k, NS) * C + j
        out_slot = lax.rem(k, 2)
        for h in range(2):
            for p in range(19):
                cy = VELOCITIES[p][1]
                if s < 3:
                    if cy == 0:
                        still[s][STILL.index(p), at, h] = halves[h][p]
                    elif cy == 1:
                        up[s][UP.index(p), at, h, 8:16, :] = halves[h][p]
                    else:
                        down[s][DOWN.index(p), at, h, 0:8, :] = halves[h][p]
                elif cy == 0:
                    out_still[out_slot, STILL.index(p), j, h] = halves[h][p]
                elif cy == 1:
                    out_up[out_slot, UP.index(p), j, h] = halves[h][p]
                else:
                    out_down[out_slot, DOWN.index(p), j, h] = halves[h][p]

    def compute(work):
        tasks = [(s, k, j) for s, k in work for j in range(C)]
        fetched = []
        packed = None
        for n, (s, k, j) in enumerate(tasks):
            while len(fetched) < min(n + LOOK + 1, len(tasks)):
                fetched.append(fetch(*tasks[len(fetched)]))
            halves = [collide(fetched[n][h], tau_g, rate36, keep, half_keep) for h in range(2)]
            column = turn(push(halves, lanes), 2 * j)
            packed = column if j == 0 else jnp.where(places >= 2 * j, column, packed)
            keep_plane(s, k, j, halves)
            if j == C - 1:
                if s < 3:
                    zsend[s][lax.rem(k, NS)] = packed
                else:
                    out_z[lax.rem(k, NZ)] = packed
                send(s, k)

    def send(s, k):
        if s < 3:
            for copy in sends(s, lax.rem(k, NS)):
                copy.start()
        else:
            for copy in writes(k, lax.rem(k, 2)) + z_sends(k):
                copy.start()
            face_moves(k, lambda copy, remote: copy.start())

    def arrive(s, k):
        if s == 0:
            load(k, lax.rem(k, 2)).wait()
        else:
            settle(recv_sem.at[s - 1, lax.rem(k + 1, NS)], GROUP_ROWS)

    def reclaim(s, k):
        if s < 3:
            settle(send_sem.at[s, lax.rem(k, NS)], GROUP_ROWS)
        else:
            for copy in writes(k - 2, lax.rem(k, 2)):
                copy.wait()
            face_reclaim(k - 2)

    def stage(s, i):
        k = i - s * LAG
        last = chunks if s < 3 else chunks - 1

        @pl.when((k >= 0) & (k <= last))
        def _():
            if s > 0:
                @pl.when(k == 0)
                def _():
                    arrive(s, -1)
            pl.when(k < chunks + (s == 0))(lambda: arrive(s, k))
            pl.when(k >= (NS if s < 3 else 2))(lambda: reclaim(s, k))
            if s == 0:
                pl.when(k == 0)(lambda: pl.semaphore_wait(barrier, 5))
            if s == 3:
                pl.when(k >= NZ)(lambda: settle(zsend_sem.at[lax.rem(k, NZ)], Z_ROWS))
                pl.when(k >= ZLAG)(lambda: settle(zrecv_sem.at[lax.rem(k - ZLAG, NZ)], Z_ROWS))
            compute([(s, k)])
            if s == 0:
                pl.when(k + 2 <= chunks)(lambda: load(k + 2, lax.rem(k, 2)).start())

    def step(i, carry):
        for s in range(STEPS):
            stage(s, i)
        return carry

    lax.fori_loop(0, chunks + 3 * LAG, step, 0)

    def repeat(low, high, wait):
        def one(n, carry):
            wait(n)
            return carry

        lax.fori_loop(low, high, one, 0)

    for s in range(STEPS - 1):
        repeat(0, NS, lambda slot: settle(send_sem.at[s, slot], GROUP_ROWS))
    repeat(chunks - ZLAG, chunks, lambda k: settle(zrecv_sem.at[lax.rem(k, NZ)], Z_ROWS))
    last = pltpu.make_async_copy(in_z, z_halo, in_sem.at[0])
    last.start()
    repeat(0, NZ, lambda slot: settle(zsend_sem.at[slot], Z_ROWS))
    for k in (chunks - 2, chunks - 1):
        for copy in writes(k, k % 2):
            copy.wait()
        face_reclaim(k)

    def face_arrive(k):
        face_moves(k, lambda copy, remote: copy.wait_recv(), 1)

    repeat(0, PIECES[0] + 1, face_arrive)
    last.wait()


def face_spans(chunks):
    spans = []
    base = 0
    for n, count in enumerate(PIECES):
        high = base + count + 1
        spans.append((n, base, min(high, chunks), base))
        if high > chunks:
            spans.append((n, 0, high - chunks, base - chunks))
        base += count
    return spans


def march(relax_time, body_force, populations):
    nx = populations.shape[1]
    chunks = nx // C
    state = [jax.ShapeDtypeStruct((pops, nx, 2) + TILE, F32) for pops in GROUPS]
    halo_z = (chunks, 3 * TILE[0], TILE[1])
    faces = [
        jax.ShapeDtypeStruct((pops, (count + 1) * C, 2, TILE[1]), F32) for count in PIECES for pops in GROUPS[1:]]
    anywhere = pl.BlockSpec(memory_space=pl.ANY)
    outs = state + [jax.ShapeDtypeStruct(halo_z, F32)] + faces
    dma = pltpu.SemaphoreType.DMA
    stages = STEPS - 1
    wide = 2 * TILE[0]
    return pl.pallas_call(
        functools.partial(march_kernel, chunks),
        out_shape=outs,
        in_specs=[pl.BlockSpec(memory_space=pltpu.SMEM)] * 2 + [anywhere],
        out_specs=[anywhere] * len(outs),
        scratch_shapes=[
            pltpu.VMEM((2, populations.shape[0], C) + populations.shape[2:], F32),
            [
                [ring(GROUPS[0], RP)] * stages, [ring(GROUPS[1], RP, wide)] * stages, [ring(GROUPS[2], RP, wide)] * stages,
                [pltpu.VMEM((NS,) + TILE, F32)] * stages, [pltpu.VMEM((NS,) + halo_z[1:], F32)] * stages,
            ],
            *[pltpu.VMEM((2, pops, C, 2) + TILE, F32) for pops in GROUPS],
            pltpu.VMEM((NZ,) + TILE, F32), pltpu.VMEM(halo_z, F32),
            dma((2,)), dma((2, 3)), dma((2, 2, 2)), dma((stages, NS)), dma((stages, NS)), dma((NZ,)), dma((NZ,)),
            dma((2, 2)), dma((PIECES[0] + 1, 2)),
            pltpu.VMEM((GROUP_ROWS, TILE[1]), F32),
        ],
        compiler_params=pltpu.CompilerParams(collective_id=0, has_side_effects=True, vmem_limit_bytes=VMEM_BYTES),
        cost_estimate=pl.CostEstimate(flops=10 ** 9, bytes_accessed=10 ** 8, transcendentals=0),
        name="march",
    )(relax_time, body_force, populations)


KW = 3
KR = 4


def final_kernel(
    first, count, aliased, tau_ref, force_ref, g_still, g_up, g_down, halo_up, halo_down, z_in, *rest,
):
    rest = rest[3:] if aliased else rest
    pops, density, velocity, still, up, down, zs, out_f, out_m, in_sem, out_sem, z_sem = rest
    chunks = g_still.shape[1] // C
    tau = splat(tau_ref[0])
    tau_g = tuple(tau * force_ref[axis] for axis in range(3))
    lanes = lax.broadcasted_iota(jnp.int32, TILE, 1)

    z_copy = pltpu.make_async_copy(z_in, zs, z_sem)
    z_copy.start()

    def state_loads(t):
        slot = lax.rem(t, KR)
        src = pl.ds(lax.rem(first + t + chunks - 1, chunks) * C, C)
        dst = pl.ds(slot * C, C)
        return [
            pltpu.make_async_copy(g_still.at[:, src], still.at[:, dst], in_sem.at[slot, 0]),
            pltpu.make_async_copy(g_up.at[:, src], up.at[:, dst, :, 8:16], in_sem.at[slot, 1]),
            pltpu.make_async_copy(g_down.at[:, src], down.at[:, dst, :, 0:8], in_sem.at[slot, 2]),
        ]

    def halo_loads(t, skip, size):
        slot = lax.rem(t, KR)
        src = pl.ds(t * C + skip, size)
        dst = pl.ds(slot * C + skip, size)
        return [
            pltpu.make_async_copy(halo_up.at[:, src], up.at[:, dst, :, 7], in_sem.at[slot, 3]),
            pltpu.make_async_copy(halo_down.at[:, src], down.at[:, dst, :, 8], in_sem.at[slot, 4]),
        ]

    def loads(t, act):
        for copy in state_loads(t):
            act(copy)
        for cond, skip, size in ((t == 0, 4, 4), ((t > 0) & (t < count), 0, C), (t == count, 0, 6)):
            @pl.when(cond)
            def _():
                for copy in halo_loads(t, skip, size):
                    act(copy)

    def writes(t):
        slot = lax.rem(t, KW)
        dst = pl.ds(lax.rem(first + t - 1, chunks) * C, C)
        return [
            pltpu.make_async_copy(out_f.at[slot], pops.at[:, dst], out_sem.at[slot, 0]),
            pltpu.make_async_copy(out_m.at[slot, 0], density.at[dst], out_sem.at[slot, 1]),
            pltpu.make_async_copy(out_m.at[slot, pl.ds(1, 3)], velocity.at[:, dst], out_sem.at[slot, 2]),
        ]

    start = lambda copy: copy.start()
    finish = lambda copy: copy.wait()
    for t in range(3):
        loads(t, start)
    loads(0, finish)
    z_copy.wait()

    def step(t, carry):
        @pl.when(t + 2 <= count)
        def _():
            loads(t + 2, start)

        loads(t, finish)

        @pl.when(t > KW)
        def _():
            for copy in writes(t - KW):
                copy.wait()

        slot = lax.rem(t, KW)

        for j in range(C):
            planes = {}
            chunk = {}
            for cx in (1, 0, -1):
                ahead, place = divmod(5 + j - cx, C)
                planes[cx] = (lax.rem(t - 1 + ahead, KR) * C + place, place)
                chunk[cx] = lax.rem(first - 2 + ahead + t + chunks, chunks)
            zhalo = lambda cx, rows: zs[chunk[cx], rows, :]
            halves = pull(still, up, down, zhalo, planes, lanes)
            for h in range(2):
                f = halves[h]
                rho, u = forced_moments(f, tau_g)
                window = slice(128 * h, 128 * h + 128)
                for p in range(19):
                    out_f[slot, p, j, :, window] = f[p]
                for n, value in enumerate((rho,) + u):
                    out_m[slot, n, j, :, window] = value
        for copy in writes(t):
            copy.start()
        return carry

    lax.fori_loop(1, count + 1, step, 0)
    for t in range(count + 1 - KW, count + 1):
        for copy in writes(t):
            copy.wait()


def final(first, count, relax_time, body_force, state, halos, outs):
    nx = state[0].shape[1]
    chunks = nx // C
    anywhere = pl.BlockSpec(memory_space=pl.ANY)
    aliased = outs is not None
    operands = (relax_time, body_force) + state + halos + (outs if aliased else ())
    base = len(operands) - 3
    block = (TILE[0], 2 * TILE[1])
    dma = pltpu.SemaphoreType.DMA
    wide = 2 * TILE[0]
    return pl.pallas_call(
        functools.partial(final_kernel, first, count, aliased),
        out_shape=tuple(jax.ShapeDtypeStruct(lead + (nx,) + block, F32) for lead in ((sum(GROUPS),), (), (3,))),
        in_specs=[pl.BlockSpec(memory_space=pltpu.SMEM)] * 2 + [anywhere] * (len(operands) - 2),
        out_specs=(anywhere,) * 3,
        input_output_aliases={base + n: n for n in range(3)} if aliased else {},
        scratch_shapes=[
            ring(GROUPS[0], KR * C), ring(GROUPS[1], KR * C, wide), ring(GROUPS[2], KR * C, wide),
            pltpu.VMEM((chunks, 3 * TILE[0], TILE[1]), F32),
            pltpu.VMEM((KW, sum(GROUPS), C) + block, F32), pltpu.VMEM((KW, 4, C) + block, F32),
            dma((KR, 5)), dma((KW, 3)), dma,
        ],
        compiler_params=pltpu.CompilerParams(vmem_limit_bytes=48 * 2 ** 20),
        cost_estimate=pl.CostEstimate(flops=count * 10 ** 6, bytes_accessed=count * 3 * 10 ** 6, transcendentals=0),
        name="final",
    )(*operands)


def solution(mesh):
    size_y = mesh.shape["py"]
    size_z = mesh.shape["pz"]
    field_spec = P(None, None, "py", "pz")

    def shift(block, dy, dz):
        pairs = []
        for z in range(size_z):
            for y in range(size_y):
                pairs.append((z * size_y + y, (z + dz) % size_z * size_y + (y + dy) % size_y))
        return lax.ppermute(block, ("pz", "py"), pairs)

    def local_steps(populations, relax_time, body_force):
        tau = relax_time.reshape((1,))
        *state, z_halo = (marched := march(tau, body_force, populations))[:4]
        faces = marched[4:]
        outs = None
        first = 1
        for n, count in enumerate(PIECES):
            up, down = faces[2 * n:2 * n + 2]
            if n:
                up = shift(up, 1, 0)
                down = shift(down, -1, 0)
            outs = final(first, count, tau, body_force, tuple(state), (up, down, z_halo), outs)
            first += count
        return tuple(outs)

    return jax.shard_map(local_steps, mesh=mesh, in_specs=(field_spec, P(), P()), out_specs=(field_spec, P(None, "py", "pz"), field_spec), check_vma=False)
```

time: 3690 us -> 318 us (0.09)
  local copies, waits for them, and re-layouts: 1460 us -> 3.17 us
  other arithmetic: 1440 us -> 0 us
  waiting for transfers between devices: 763 us -> 20.5 us
  Pallas kernels: 0 us -> 286 us
    slice x27 -> x0, local copies, waits for them, and re-layouts: 1020 us -> none  [the longest x8 588 us: neighbour_planes(): lower = lax.slice_in_dim(block, 0, depth, axis=dim)]
    ppermute x16 -> x8, waiting for transfers between devices: 763 us -> 20.5 us  [shift(): return lax.ppermute(block, ('pz', 'py'), pairs)]
    unnamed x81 -> x0, other arithmetic: 448 us -> none
    concatenate x4 -> x0, other arithmetic: 345 us -> none  [neighbour_planes(): return jnp.concatenate([from_below, block, from_above], axis=dim)]
    ppermute x8 -> x0, local copies, waits for them, and re-layouts: 304 us -> none  [the longest x4 153 us: neighbour_planes(): from_below = lax.ppermute(upper, axis_name, forward)]
    sub x9 -> x0, other arithmetic: 290 us -> none  [collide(): populations[pop_id] - (populations[pop_id] - feq_list[pop_id]) * relax_rate]
    pallas_call x0 -> x6, Pallas kernels: none -> 286 us  [the longest x1 215 us: march(): pl.pallas_call(functools.partial(march_kernel, chunks), out_shape=outs, i...]
    slice x16 -> x0, other arithmetic: 150 us -> none  [propagate_inner(): moved_pop = jnp.roll(moved_pop, shift_x, axis=0)]
  transfers between devices with their start and end apart: 16 -> 8, of which waited for: 8 -> 4; matrix products, arithmetic and copies ran while one was open for 13% -> 0% of each run, Pallas kernels for 0% -> 17%
where the time goes in v1:
time: 318 us; the launch traced here: 317 us
  Pallas kernels  286 us (90%)
  waiting for transfers between devices  20.5 us (6%)
  starting transfers between devices  6.22 us (2%)
    pallas_call x1, Pallas kernels, march(): pl.pallas_call(functools.partial(march_kernel, chunks), out_shape=outs, i...  215 us
    pallas_call x5, Pallas kernels, final(): pl.pallas_call(functools.partial(final_kernel, first, count, aliased), ou...  71.2 us
    ppermute x8, waiting for transfers between devices, shift(): return lax.ppermute(block, ('pz', 'py'), pairs)  20.5 us
  transfers between devices with their start and end apart: 8, of which 4 were waited for; matrix products, arithmetic and copies ran while one was open for 0% of the time, Pallas kernels for 17%

profile of v1, /device:TPU:0, one launch (start us, length us, event | category | flops | bytes accessed | tf_op | source)
XLA Modules:
  0.0 317.2 jit_solution(7733035372038200258)
XLA Ops:
  1.3 214.7 %march.1 = (f32[9,512,2,8,128]{4,3,2,1,0:T(8,128)}, f32[5,512,2,8,128]{4,3,2,1,0:T(8,128)}, f32[5,512,2,8,128]{4,3,2,1,0:T(8,128)}, f32[64,24,128]{2,1,0:T(8,128...) custom-call(f32[1]{0:T(128)} %bitcast.1.tau_ref, ...), custom_call_target="tpu_custom_call" | custom-call | flops 1000000000 | bytes 100000000 | tf_op jit(solution)/shard_map/march/pallas_call | solution.py:397
  216.0 0.9 collective-permute-start.6
  216.9 0.9 collective-permute-start.7
  217.8 0.0 collective-permute-start.4
  217.8 1.7 collective-permute-start.2
  219.5 0.0 collective-permute-start.3
  219.5 7.4 %collective-permute-done.6.halo_up = f32[5,88,2,128]{3,2,1,0:T(2,128)S(1)} collective-permute-done((f32[5,88,2,128]{3,2,1,0:T(2,128)}, f32[5,88,2,128]{3,2,1,0:T(2,128)S(1)}, u32[]{:S(2)}, u32[]{:S(2)}) %collective-permute-start.6) | collective-permute-done | bytes 450592 | tf_op jit(solution)/shard_map/ppermute | solution.py:560
  227.0 0.6 collective-permute-start
  227.5 1.3 collective-permute-done.7.halo_down
  228.8 2.1 collective-permute-start.1
  230.9 7.4 %collective-permute-done.4.halo_up = f32[5,104,2,128]{3,2,1,0:T(2,128)S(1)} collective-permute-done((f32[5,104,2,128]{3,2,1,0:T(2,128)}, f32[5,104,2,128]{3,2,1,0:T(2,128)S(1)}, u32[]{:S(2)}, u32[]{:S(2)}) %collective-permute-start.4) | collective-permute-done | bytes 532512 | tf_op jit(solution)/shard_map/ppermute | solution.py:560
  238.4 0.0 collective-permute-start.5
  238.4 1.1 copy-done
  239.5 1.0 copy-done.1
  240.5 1.0 copy-done.2
  241.5 11.8 %final.5 = (f32[19,512,8,256]{3,2,1,0:T(8,128)}, f32[512,8,256]{2,1,0:T(8,128)}, f32[3,512,8,256]{3,2,1,0:T(8,128)}) custom-call(f32[1]{0:T(128)} %bitcast.2.tau_ref, f32[3]{0:T(128)S(1)} %copy-done.3, f32[9,512,2,8,128]{4,3,2,1,0:T(8,128)} %get-tuple-element.29.g_still, f32[5,512,2,8,128]{4,3,2,1,0:T(8,128)} %get-tuple-element.30.g_up, ...), custom_call_target="tpu_custom_call" | custom-call | flops 10000000 | bytes 30000000 | tf_op jit(solution)/shard_map/final/pallas_call | solution.py:532
  253.3 11.7 %final.6 = (f32[19,512,8,256]{3,2,1,0:T(8,128)}, f32[512,8,256]{2,1,0:T(8,128)}, f32[3,512,8,256]{3,2,1,0:T(8,128)}) custom-call(f32[1]{0:T(128)} %bitcast.3.tau_ref, f32[3]{0:T(128)S(1)} %copy-done.3, f32[9,512,2,8,128]{4,3,2,1,0:T(8,128)} %get-tuple-element.29.g_still, ...), custom_call_target="tpu_custom_call", output_to_operand_aliasing={{0}: (8, {}), {1}: (9, {}), {2}: (10, {})} | custom-call | flops 10000000 | bytes 30000000 | tf_op jit(solution)/shard_map/final/pallas_call | solution.py:532
  265.0 4.4 %collective-permute-done.5.halo_down = f32[5,104,2,128]{3,2,1,0:T(2,128)S(1)} collective-permute-done((f32[5,104,2,128]{3,2,1,0:T(2,128)}, f32[5,104,2,128]{3,2,1,0:T(2,128)S(1)}, u32[]{:S(2)}, u32[]{:S(2)}) %collective-permute-start.5) | collective-permute-done | bytes 532512 | tf_op jit(solution)/shard_map/ppermute | solution.py:560
  269.4 13.3 %final.7 = (f32[19,512,8,256]{3,2,1,0:T(8,128)}, f32[512,8,256]{2,1,0:T(8,128)}, f32[3,512,8,256]{3,2,1,0:T(8,128)}) custom-call(f32[1]{0:T(128)} %bitcast.4.tau_ref, f32[3]{0:T(128)S(1)} %copy-done.3, f32[9,512,2,8,128]{4,3,2,1,0:T(8,128)} %get-tuple-element.29.g_still, ...), custom_call_target="tpu_custom_call", output_to_operand_aliasing={{0}: (8, {}), {1}: (9, {}), {2}: (10, {})} | custom-call | flops 12000000 | bytes 36000000 | tf_op jit(solution)/shard_map/final/pallas_call | solution.py:532
  282.7 0.0 collective-permute-done.2.halo_up
  282.7 0.0 collective-permute-done.3.halo_down
  282.7 17.0 %final.8 = (f32[19,512,8,256]{3,2,1,0:T(8,128)}, f32[512,8,256]{2,1,0:T(8,128)}, f32[3,512,8,256]{3,2,1,0:T(8,128)}) custom-call(f32[1]{0:T(128)} %bitcast.5.tau_ref, f32[3]{0:T(128)S(1)} %copy-done.3, f32[9,512,2,8,128]{4,3,2,1,0:T(8,128)} %get-tuple-element.29.g_still, ...), custom_call_target="tpu_custom_call", output_to_operand_aliasing={{0}: (8, {}), {1}: (9, {}), {2}: (10, {})} | custom-call | flops 16000000 | bytes 48000000 | tf_op jit(solution)/shard_map/final/pallas_call | solution.py:532
  299.7 0.0 collective-permute-done.1.halo_down
  299.7 17.5 %final.9 = (f32[19,512,8,256]{3,2,1,0:T(8,128)}, f32[512,8,256]{2,1,0:T(8,128)}, f32[3,512,8,256]{3,2,1,0:T(8,128)}) custom-call(f32[1]{0:T(128)} %bitcast.6.tau_ref, f32[3]{0:T(128)S(1)} %copy-done.3, f32[9,512,2,8,128]{4,3,2,1,0:T(8,128)} %get-tuple-element.29.g_still, ...), custom_call_target="tpu_custom_call", output_to_operand_aliasing={{0}: (8, {}), {1}: (9, {}), {2}: (10, {})} | custom-call | flops 16000000 | bytes 48000000 | tf_op jit(solution)/shard_map/final/pallas_call | solution.py:532
  (6 shorter events, 0.0 us)
Async XLA Ops:
  1.3 237.1 %copy-start.3 = (f32[3]{0:T(128)S(1)}, f32[3]{0:T(128)}, u32[]{:S(2)}) copy-start(f32[3]{0:T(128)} %force_ref.11) | copy-start | bytes 40
  216.0 11.0 %collective-permute-start.6 = (f32[5,88,2,128]{3,2,1,0:T(2,128)}, f32[5,88,2,128]{3,2,1,0:T(2,128)S(1)}, u32[]{:S(2)}, u32[]{:S(2)}) collective-permute-start(f32[5,88,2,128]{3,2,1,0:T(2,128)} %get-tuple-element.39), channel_id=1, source_target_pairs={{0,1},{1,2},{2,3},{3,0},{4,5},{5,6},{6,7},{7,4}} | collective-permute-start | bytes 1351688 | tf_op jit(solution)/shard_map/ppermute | solution.py:560
  216.9 12.0 %collective-permute-start.7 = (f32[5,88,2,128]{3,2,1,0:T(2,128)}, f32[5,88,2,128]{3,2,1,0:T(2,128)S(1)}, u32[]{:S(2)}, u32[]{:S(2)}) collective-permute-start(f32[5,88,2,128]{3,2,1,0:T(2,128)} %get-tuple-element.40), channel_id=1, source_target_pairs={{0,3},{1,0},{2,1},{3,2},{4,7},{5,4},{6,5},{7,6}} | collective-permute-start | bytes 1351688 | tf_op jit(solution)/shard_map/ppermute | solution.py:560
  217.8 20.6 %collective-permute-start.4 = (f32[5,104,2,128]{3,2,1,0:T(2,128)}, f32[5,104,2,128]{3,2,1,0:T(2,128)S(1)}, u32[]{:S(2)}, u32[]{:S(2)}) collective-permute-start(f32[5,104,2,128]{3,2,1,0:T(2,128)} %get-tuple-element.37), channel_id=1, source_target_pairs={{0,1},{1,2},{2,3},{3,0},{4,5},{5,6},{6,7},{7,4}} | collective-permute-start | bytes 1597448 | tf_op jit(solution)/shard_map/ppermute | solution.py:560
  217.8 64.9 %collective-permute-start.2 = (f32[5,136,2,128]{3,2,1,0:T(2,128)}, f32[5,136,2,128]{3,2,1,0:T(2,128)S(1)}, u32[]{:S(2)}, u32[]{:S(2)}) collective-permute-start(f32[5,136,2,128]{3,2,1,0:T(2,128)} %get-tuple-element.35), channel_id=1, source_target_pairs={{0,1},{1,2},{2,3},{3,0},{4,5},{5,6},{6,7},{7,4}} | collective-permute-start | bytes 2088968 | tf_op jit(solution)/shard_map/ppermute | solution.py:560
  219.5 63.2 %collective-permute-start.3 = (f32[5,136,2,128]{3,2,1,0:T(2,128)}, f32[5,136,2,128]{3,2,1,0:T(2,128)S(1)}, u32[]{:S(2)}, u32[]{:S(2)}) collective-permute-start(f32[5,136,2,128]{3,2,1,0:T(2,128)} %get-tuple-element.36), channel_id=1, source_target_pairs={{0,3},{1,0},{2,1},{3,2},{4,7},{5,4},{6,5},{7,6}} | collective-permute-start | bytes 2088968 | tf_op jit(solution)/shard_map/ppermute | solution.py:560
  227.0 72.8 %collective-permute-start = (f32[5,136,2,128]{3,2,1,0:T(2,128)}, f32[5,136,2,128]{3,2,1,0:T(2,128)}, u32[]{:S(2)}, u32[]{:S(2)}) collective-permute-start(f32[5,136,2,128]{3,2,1,0:T(2,128)} %get-tuple-element.32), channel_id=1, source_target_pairs={{0,1},{1,2},{2,3},{3,0},{4,5},{5,6},{6,7},{7,4}} | collective-permute-start | bytes 2088968 | tf_op jit(solution)/shard_map/ppermute | solution.py:560
  228.8 70.9 %collective-permute-start.1 = (f32[5,136,2,128]{3,2,1,0:T(2,128)}, f32[5,136,2,128]{3,2,1,0:T(2,128)}, u32[]{:S(2)}, u32[]{:S(2)}) collective-permute-start(f32[5,136,2,128]{3,2,1,0:T(2,128)} %get-tuple-element.33), channel_id=1, source_target_pairs={{0,3},{1,0},{2,1},{3,2},{4,7},{5,4},{6,5},{7,6}} | collective-permute-start | bytes 2088968 | tf_op jit(solution)/shard_map/ppermute | solution.py:560
  238.4 31.0 %collective-permute-start.5 = (f32[5,104,2,128]{3,2,1,0:T(2,128)}, f32[5,104,2,128]{3,2,1,0:T(2,128)S(1)}, u32[]{:S(2)}, u32[]{:S(2)}) collective-permute-start(f32[5,104,2,128]{3,2,1,0:T(2,128)} %get-tuple-element.38), channel_id=1, source_target_pairs={{0,3},{1,0},{2,1},{3,2},{4,7},{5,4},{6,5},{7,6}} | collective-permute-start | bytes 1597448 | tf_op jit(solution)/shard_map/ppermute | solution.py:560
  238.4 1.1 copy-start
  239.5 1.0 copy-start.1
  240.5 1.0 copy-start.2
